TPU v7x, 512 devices: a 4x2x32 block of a 4x8x32 slice. The times are simulated.
512 devices in a mesh: member: 2 (over y), tile: 32 (over z), row: 4 (over x), lev: 2 (over core).
Axes of the slice: x: 4, y: 2, z: 32, core: 2. Of those that a mesh axis runs over, the one named last changes fastest.
The devices are a block of a 4x8x32 slice.
Arguments:
- thickness: float32 [128, 512, 512], P(('member', 'lev'), 'tile', 'row'), parts along dimension 0, may hold values from 0.24 to 14.91
- zonal_wind: float32 [128, 512, 512], P(('member', 'lev'), 'tile', 'row'), parts along dimension 0, may hold values from -1.8 to 1.8
- merid_wind: float32 [128, 512, 512], P(('member', 'lev'), 'tile', 'row'), parts along dimension 0, may hold values from -1.8 to 1.8
- pert_codes: int32 [1024, 512], P(('member', 'tile'), 'row'), parts along dimension 0, may hold values from 0 to 1073741823
Outputs:
- thick_out: float32 [128, 512, 512], P(('member', 'lev'), 'tile', 'row'), parts along dimension 0
- zonal_out: float32 [128, 512, 512], P(('member', 'lev'), 'tile', 'row'), parts along dimension 0
- merid_out: float32 [128, 512, 512], P(('member', 'lev'), 'tile', 'row'), parts along dimension 0
There are 2 independent parts, one for each index of `member`. A program takes and returns all parts, laid end to end along the dimension named above; each array names one. Nothing has to cross between parts.
All inputs are finite; a program needn't handle non-finite values.
Results may differ from a plain program's by a relative error of at most 0.0003.
Values sent between devices are 32-bit elements; how exact they have to be, the bound alone decides.
A program may use at most 64 MiB of HBM per device.

v0:
```python
import jax
import jax.numpy as jnp
from jax import lax
from jax.sharding import PartitionSpec as P

NSUB = 4
CFL_NUMBER = 0.8


def one_axis_at_a_time(shard, axes):
    for axis in axes:
        shard = lax.pmax(shard, axis)
    return shard


def over_axes(shard, axes):
    for axis in axes:
        shard = lax.psum(shard, axis)
    return shard


def padded(block, sides, width):
    for axis, dim in sides:
        count = lax.axis_size(axis)
        forward = [(i, i + 1) for i in range(count - 1)]
        forward.append((count - 1, 0))
        backward = [(target, source) for source, target in forward]
        low = lax.ppermute(
            lax.slice_in_dim(block, block.shape[dim] - width, None, axis=dim), axis, forward
        )
        high = lax.ppermute(lax.slice_in_dim(block, 0, width, axis=dim), axis, backward)
        block = jnp.concatenate([low, block, high], axis=dim)
    return block


def joined_along(pieces, dim):
    pieces = jnp.moveaxis(pieces, 0, dim)
    dims = pieces.shape
    return pieces.reshape(*dims[:dim], dims[dim] * dims[dim + 1], *dims[dim + 2 :])


def sent_to_all(shard, axis):
    length = lax.axis_size(axis)
    return lax.all_to_all(
        jnp.broadcast_to(shard[None], (length, *shard.shape)), axis, 0, 0, tiled=True
    )


def gathered_copies(shard, axis, dim):
    return joined_along(sent_to_all(shard, axis), dim)


def advance(stacked, half_step):
    height = stacked[0]
    zonal = stacked[1]
    merid = stacked[2]
    zonal_new = zonal[:, 1:-1, 1:-1] - half_step * (height[:, 2:, 1:-1] - height[:, :-2, 1:-1])
    merid_new = merid[:, 1:-1, 1:-1] - half_step * (height[:, 1:-1, 2:] - height[:, 1:-1, :-2])
    centre = height[:, 1:-1, 1:-1]
    flux_east = centre * zonal_new
    flux_north = centre * merid_new
    height_new = centre[:, 1:-1, 1:-1] - half_step * (
        flux_east[:, 2:, 1:-1]
        - flux_east[:, :-2, 1:-1]
        + (flux_north[:, 1:-1, 2:] - flux_north[:, 1:-1, :-2])
    )
    return jnp.stack([height_new, zonal_new[:, 1:-1, 1:-1], merid_new[:, 1:-1, 1:-1]])


def remap_columns(columns, first, count):
    height = columns[0]
    zonal = columns[1]
    merid = columns[2]
    levels = height.shape[0]
    total = jnp.sum(height, 0)
    tops = jnp.cumsum(height, 0) - height
    marks = (first + jnp.arange(count + 1)).astype(jnp.float32)
    targets = total[None] * (marks / levels)[:, None, None]
    zonal_sum = jnp.zeros(targets.shape, jnp.float32)
    merid_sum = jnp.zeros(targets.shape, jnp.float32)
    for block in range(levels // 8):
        lower = block * 8
        upper = lower + 8
        over = jnp.clip(targets[None] - tops[lower:upper, None], 0.0, height[lower:upper, None])
        zonal_sum = zonal_sum + jnp.sum(zonal[lower:upper, None] * over, 0)
        merid_sum = merid_sum + jnp.sum(merid[lower:upper, None] * over, 0)
    layer = total / levels
    thick_new = jnp.broadcast_to(layer, (count,) + layer.shape)
    zonal_new = (zonal_sum[1:] - zonal_sum[:-1]) / layer
    merid_new = (merid_sum[1:] - merid_sum[:-1]) / layer
    return jnp.stack([thick_new, zonal_new, merid_new])


def local(thickness, zonal_wind, merid_wind, pert_codes):
    bump = 2.0 * (pert_codes % 4096).astype(jnp.float32) / 4095.0
    raised = thickness + bump[None]
    local_peak = jnp.max(raised)
    base_mass = jnp.sum(thickness)
    raised_mass = jnp.sum(raised)
    peak = one_axis_at_a_time(local_peak, ("tile", "row", "lev"))
    base_total, raised_total = (
        over_axes(base_mass, ("tile", "row", "lev")),
        over_axes(raised_mass, ("tile", "row", "lev")),
    )
    height = raised * (base_total / raised_total)
    half_step = 0.5 * CFL_NUMBER / jnp.sqrt(peak)
    state = jnp.stack([height, zonal_wind, merid_wind])
    state = padded(state, (("tile", 2), ("row", 3)), 2 * NSUB)
    for substep in range(NSUB):
        state = advance(state, half_step)
    levels_here = state.shape[1]
    columns = gathered_copies(state, "lev", 1)
    result = remap_columns(columns, lax.axis_index("lev") * levels_here, levels_here)
    return (result[0], result[1], result[2])


def solution(mesh):
    in_specs = (
        P(("member", "lev"), "tile", "row"),
        P(("member", "lev"), "tile", "row"),
        P(("member", "lev"), "tile", "row"),
        P(("member", "tile"), "row"),
    )
    out_specs = (
        P(("member", "lev"), "tile", "row"),
        P(("member", "lev"), "tile", "row"),
        P(("member", "lev"), "tile", "row"),
    )
    return jax.shard_map(local, mesh=mesh, in_specs=in_specs, out_specs=out_specs, check_vma=False)
```

profile of v0, /device:TPU:33, one launch (start us, length us, event | category | flops | bytes accessed | tf_op | source)
XLA Modules:
  0.0 252.3 jit_solution(18031665177296941275)
XLA Ops:
  1.4 1.6 add_reduce_fusion
  3.0 83.6 %all-reduce = (f32[]{:T(128)}, f32[]{:T(128)}) all-reduce(f32[]{:T(128)} %get-tuple-element.33, f32[]{:T(128)} %get-tuple-element.32), channel_id=1, replica_groups=mesh['member'=2,'tile'=32,'row'=4,'lev'=2] {'tile'}, use_global_device_ids=true, to_apply=%region_1.2 | all-reduce | flops 2 | bytes 16 | tf_op jit(solution)/shard_map/psum | solution.py:18
  86.7 9.5 %all-reduce.1 = (f32[]{:T(128)}, f32[]{:T(128)}) all-reduce(f32[]{:T(128)} %get-tuple-element.34, f32[]{:T(128)} %get-tuple-element.35), channel_id=1, replica_groups=mesh['member'=2,'tile'=32,'row'=4,'lev'=2] {'row'}, use_global_device_ids=true, to_apply=%region_2.3 | all-reduce | flops 2 | bytes 16 | tf_op jit(solution)/shard_map/psum | solution.py:18
  96.2 19.4 %all-reduce.2 = (f32[]{:T(128)}, f32[]{:T(128)}) all-reduce(f32[]{:T(128)} %get-tuple-element.36, f32[]{:T(128)} %get-tuple-element.37), channel_id=1, replica_groups=mesh['member'=2,'tile'=32,'row'=4,'lev'=2] {'lev'}, use_global_device_ids=true, to_apply=%region_3.4 | all-reduce | flops 2 | bytes 16 | tf_op jit(solution)/shard_map/psum | solution.py:18
  119.0 2.0 collective-permute-start
  121.0 4.6 %collective-permute-start.1 = (f32[3,32,8,128]{3,2,1,0:T(8,128)S(1)}, f32[3,32,8,128]{3,2,1,0:T(8,128)}, u32[]{:S(2)}, u32[]{:S(2)}) collective-permute-start(f32[3,32,8,128]{3,2,1,0:T(8,128)S(1)} %get-tuple-element.74), channel_id=1, source_target_pairs={{8,0},{16,8},{24,16},{32,24},{40,32},{48,40},{56,48},{64,56},{72,6... | collective-permute-start | bytes 1179656 | tf_op jit(solution)/shard_map/ppermute | solution.py:31
  125.6 46.2 %pmax.21 = f32[]{:T(128)} all-reduce(f32[]{:T(128)} %get-tuple-element.31), channel_id=1, replica_groups=mesh['member'=2,'tile'=32,'row'=4,'lev'=2] {'tile'}, use_global_device_ids=true, to_apply=%region_9.10 | all-reduce | flops 1 | bytes 8 | tf_op jit(solution)/shard_map/pmax | solution.py:12
  171.8 6.7 %pmax.22 = f32[]{:T(128)} all-reduce(f32[]{:T(128)} %pmax.21), channel_id=1, replica_groups=mesh['member'=2,'tile'=32,'row'=4,'lev'=2] {'row'}, use_global_device_ids=true, to_apply=%region_10.11 | all-reduce | flops 1 | bytes 8 | tf_op jit(solution)/shard_map/pmax | solution.py:12
  178.5 18.6 %pmax.23 = f32[]{:T(128)} all-reduce(f32[]{:T(128)} %pmax.22), channel_id=1, replica_groups=mesh['member'=2,'tile'=32,'row'=4,'lev'=2] {'lev'}, use_global_device_ids=true, to_apply=%region_11.12 | all-reduce | flops 1 | bytes 8 | tf_op jit(solution)/shard_map/pmax | solution.py:12
  197.8 1.3 pad_maximum_fusion.1
  200.9 3.6 %collective-permute-start.2 = (f32[3,32,32,8]{2,3,1,0:T(8,128)}, f32[3,32,32,8]{2,3,1,0:T(8,128)S(1)}, u32[]{:S(2)}, u32[]{:S(2)}) collective-permute-start(f32[3,32,32,8]{2,3,1,0:T(8,128)} %copy.20), channel_id=1, source_target_pairs={{0,2},{2,4},{4,6},{6,0},{1,3},{3,5},{5,7},{7,1},{8,10},{10,12},{12... | collective-permute-start | bytes 294920 | tf_op jit(solution)/shard_map/ppermute | solution.py:28
  205.0 3.1 %collective-permute-start.3 = (f32[3,32,32,8]{2,3,1,0:T(8,128)S(1)}, f32[3,32,32,8]{2,3,1,0:T(8,128)}, u32[]{:S(2)}, u32[]{:S(2)}) collective-permute-start(f32[3,32,32,8]{2,3,1,0:T(8,128)S(1)} %copy.21), channel_id=1, source_target_pairs={{2,0},{4,2},{6,4},{0,6},{3,1},{5,3},{7,5},{1,7},{10,8},{12,10},{14... | collective-permute-start | bytes 294920 | tf_op jit(solution)/shard_map/ppermute | solution.py:31
  208.1 6.5 %collective-permute-done.2 = f32[3,32,32,8]{2,3,1,0:T(8,128)S(1)} collective-permute-done((f32[3,32,32,8]{2,3,1,0:T(8,128)}, f32[3,32,32,8]{2,3,1,0:T(8,128)S(1)}, u32[]{:S(2)}, u32[]{:S(2)}) %collective-permute-start.2) | collective-permute-done | bytes 98336 | tf_op jit(solution)/shard_map/ppermute | solution.py:28
  215.1 2.0 collective-permute-done.3
  217.1 1.5 copy.19
  218.6 2.6 %pad_maximum_fusion = f32[3,32,32,144]{3,2,1,0:T(8,128)S(1)} fusion(f32[3,32,32,8]{3,2,1,0:T(8,128)S(1)} %copy.19, f32[3,32,8,128]{3,2,1,0:T(8,128)} %collective-permute-done.1, f32[1,32,16,128]{3,2,1,0:T(8,128)} %bitcast.26, f32[1,32,16,128]{3,2,1,0:T(8,128)} %bitcast.29, f32[1,32,16,128]{3,2,1,0:T(8,128)S(1)} %multiply_bitcast_fusion, ...), kind=kLoop, calls=%fused_computation | loop fusion | flops 2654208 | bytes 3538944 | tf_op jit(solution)/shard_map/concatenate | solution.py:32
  221.5 1.7 slice_multiply_fusion.3
  224.4 1.7 slice_multiply_fusion.1
  227.0 1.3 slice_multiply_fusion.7
  229.2 1.3 slice_multiply_fusion.5
  231.3 6.2 %all_to_all.5 = f32[2,3,32,16,128]{4,3,2,1,0:T(8,128)S(1)} all-to-all(f32[2,3,32,16,128]{4,3,2,1,0:T(8,128)S(1)} %broadcast_in_dim.2), channel_id=1, replica_groups=mesh['member'=2,'tile'=32,'row'=4,'lev'=2] {'lev'}, dimensions={0} | all-to-all | bytes 3145728 | tf_op jit(solution)/shard_map/all_to_all | solution.py:44
  237.7 6.9 %bitcast_subtract_fusion = f32[64,16,128]{2,1,0:T(8,128)S(1)} fusion(f32[1,2,32,16,128]{4,3,2,0,1:T(8,128)S(1)} %get-tuple-element.62, f32[64,16,128]{2,1,0:T(8,128)S(1)} %bitcast.22), kind=kOutput, calls=%fused_computation.104 | output fusion | flops 8388608 | bytes 1572864 | tf_op jit(solution)/shard_map/jit(cumsum)/reduce_window_sum | solution.py:76
  245.0 2.7 %multiply_reduce_fusion.7 = (f32[33,16,128]{2,1,0:T(8,128)S(1)}, f32[33,16,128]{2,1,0:T(8,128)S(1)}, f32[33,16,128]{2,1,0:T(8,128)S(1)}, f32[33,16,128]{2,1,0:T(...) fusion(f32[8,16,128]{2,1,0:T(8,128)S(1)} %get-tuple-element.82,, ...), kind=kLoop, calls=%fused_computation.8 | loop fusion | flops 14598144 | bytes 3481600 | tf_op jit(solution)/shard_map/reduce_sum | solution.py:86
  247.6 2.7 %multiply_reduce_fusion.6 = (f32[33,16,128]{2,1,0:T(8,128)S(1)}, f32[33,16,128]{2,1,0:T(8,128)S(1)}, f32[33,16,128]{2,1,0:T(8,128)S(1)}, f32[33,16,128]{2,1,0:T(...) fusion(f32[8,16,128]{2,1,0:T(8,128)S(1)} %get-tuple-element.81,, ...), kind=kLoop, calls=%fused_computation.7 | loop fusion | flops 14598144 | bytes 3481600 | tf_op jit(solution)/shard_map/reduce_sum | solution.py:86
  (34 shorter events, 12.2 us)
Async XLA Ops:
  0.6 197.2 %copy-start.1 = (f32[32,16,128]{2,1,0:T(8,128)S(1)}, f32[32,16,128]{2,1,0:T(8,128)}, u32[]{:S(2)}) copy-start(f32[32,16,128]{2,1,0:T(8,128)} %param.5) | copy-start | bytes 786436
  0.6 197.2 %copy-start = (f32[32,16,128]{2,1,0:T(8,128)S(1)}, f32[32,16,128]{2,1,0:T(8,128)}, u32[]{:S(2)}) copy-start(f32[32,16,128]{2,1,0:T(8,128)} %param.6) | copy-start | bytes 786436
  119.0 78.7 %collective-permute-start = (f32[3,32,8,128]{3,2,1,0:T(8,128)S(1)}, f32[3,32,8,128]{3,2,1,0:T(8,128)}, u32[]{:S(2)}, u32[]{:S(2)}) collective-permute-start(f32[3,32,8,128]{3,2,1,0:T(8,128)S(1)} %get-tuple-element.73), channel_id=1, source_target_pairs={{0,8},{8,16},{16,24},{24,32},{32,40},{40,48},{48,56},{56,64},{64,7... | collective-permute-start | bytes 1179656 | tf_op jit(solution)/shard_map/ppermute | solution.py:28
  121.0 76.8 %collective-permute-start.1 = (f32[3,32,8,128]{3,2,1,0:T(8,128)S(1)}, f32[3,32,8,128]{3,2,1,0:T(8,128)}, u32[]{:S(2)}, u32[]{:S(2)}) collective-permute-start(f32[3,32,8,128]{3,2,1,0:T(8,128)S(1)} %get-tuple-element.74), channel_id=1, source_target_pairs={{8,0},{16,8},{24,16},{32,24},{40,32},{48,40},{56,48},{64,56},{72,6... | collective-permute-start | bytes 1179656 | tf_op jit(solution)/shard_map/ppermute | solution.py:31
  200.9 13.7 %collective-permute-start.2 = (f32[3,32,32,8]{2,3,1,0:T(8,128)}, f32[3,32,32,8]{2,3,1,0:T(8,128)S(1)}, u32[]{:S(2)}, u32[]{:S(2)}) collective-permute-start(f32[3,32,32,8]{2,3,1,0:T(8,128)} %copy.20), channel_id=1, source_target_pairs={{0,2},{2,4},{4,6},{6,0},{1,3},{3,5},{5,7},{7,1},{8,10},{10,12},{12... | collective-permute-start | bytes 294920 | tf_op jit(solution)/shard_map/ppermute | solution.py:28
  205.0 12.1 %collective-permute-start.3 = (f32[3,32,32,8]{2,3,1,0:T(8,128)S(1)}, f32[3,32,32,8]{2,3,1,0:T(8,128)}, u32[]{:S(2)}, u32[]{:S(2)}) collective-permute-start(f32[3,32,32,8]{2,3,1,0:T(8,128)S(1)} %copy.21), channel_id=1, source_target_pairs={{2,0},{4,2},{6,4},{0,6},{3,1},{5,3},{7,5},{1,7},{10,8},{12,10},{14... | collective-permute-start | bytes 294920 | tf_op jit(solution)/shard_map/ppermute | solution.py:31
where the time goes:
time: 253 us; the launch traced here: 252 us
  blocking collectives  190 us (75%)
  other arithmetic  31.5 us (12%)
  starting transfers between devices  13.3 us (5%)
  waiting for transfers between devices  8.47 us (3%)
  local copies, waits for them, and re-layouts  5.87 us (2%)
  between operations  2.96 us (1%)
    psum x3, blocking collectives, over_axes(): shard = lax.psum(shard, axis)  113 us
    pmax x3, blocking collectives, one_axis_at_a_time(): shard = lax.pmax(shard, axis)  71.5 us
    ppermute x2, starting transfers between devices, padded(): lax.ppermute(lax.slice_in_dim(block, 0, width, axis=dim), axis, backward)  7.7 us
    another operation x1, other arithmetic, remap_columns(): tops = jnp.cumsum(height, 0) - height  6.88 us
    ppermute x2, waiting for transfers between devices, padded(): lax.ppermute(lax.slice_in_dim(block, block.shape[dim] - width, None, axis...  6.46 us
    all_to_all x1, blocking collectives, sent_to_all(): lax.all_to_all(jnp.broadcast_to(shard[None], (length, *shard.shape)), axi...  6.23 us
    mul x4, other arithmetic, advance(): flux_east = centre * zonal_new  5.99 us
    ppermute x2, starting transfers between devices, padded(): lax.ppermute(lax.slice_in_dim(block, block.shape[dim] - width, None, axis...  5.58 us
  transfers between devices with their start and end apart: 4, of which 2 were waited for; matrix products, arithmetic and copies ran while one was open for 0% of the time, Pallas kernels for 0%

commit v1 on v0

--- a/solution.py
+++ b/solution.py
@@ -15,7 +15,7 @@
 
 def over_axes(shard, axes):
     for axis in axes:
-        shard = lax.psum(shard, axis)
+        shard = jnp.sum(lax.all_gather(shard, axis), axis=0)
     return shard
 
 

time: 253 us -> 269 us (1.063)
  local copies, waits for them, and re-layouts: 5.87 us -> 18.2 us
  other arithmetic: 31.5 us -> 35.2 us
  waiting for transfers between devices: 8.47 us -> 11.3 us
    psum x3 -> x0, blocking collectives: 113 us -> none  [over_axes(): shard = lax.psum(shard, axis)]
    unnamed x0 -> x3, blocking collectives: none -> 111 us
    unnamed x6 -> x21, local copies, waits for them, and re-layouts: 1.71 us -> 14 us
    ppermute x2, waiting for transfers between devices: 6.46 us -> 11.2 us  [padded(): lax.ppermute(lax.slice_in_dim(block, block.shape[dim] - width, None, axis...]
    reduce_sum x0 -> x6, other arithmetic: none -> 3.69 us  [over_axes(): shard = jnp.sum(lax.all_gather(shard, axis), axis=0)]
  transfers between devices with their start and end apart: 4 -> 4, of which waited for: 2 -> 1; matrix products, arithmetic and copies ran while one was open for 0% -> 0% of each run, Pallas kernels for 0% -> 0%
where the time goes in v1:
time: 269 us; the launch traced here: 268 us
  blocking collectives  188 us (70%)
  other arithmetic  35.2 us (13%)
  local copies, waits for them, and re-layouts  18.2 us (7%)
  starting transfers between devices  12.3 us (5%)
  waiting for transfers between devices  11.3 us (4%)
  between operations  2.98 us (1%)
    unnamed x3, blocking collectives  111 us
    pmax x3, blocking collectives, one_axis_at_a_time(): shard = lax.pmax(shard, axis)  71.5 us
    unnamed x21, local copies, waits for them, and re-layouts  14 us
    ppermute x2, waiting for transfers between devices, padded(): lax.ppermute(lax.slice_in_dim(block, block.shape[dim] - width, None, axis...  11.2 us
    ppermute x2, starting transfers between devices, padded(): lax.ppermute(lax.slice_in_dim(block, 0, width, axis=dim), axis, backward)  8.25 us
    another operation x1, other arithmetic, remap_columns(): tops = jnp.cumsum(height, 0) - height  6.88 us
    all_to_all x1, blocking collectives, sent_to_all(): lax.all_to_all(jnp.broadcast_to(shard[None], (length, *shard.shape)), axi...  6.23 us
    mul x4, other arithmetic, advance(): flux_east = centre * zonal_new  5.99 us
  transfers between devices with their start and end apart: 4, of which 1 were waited for; matrix products, arithmetic and copies ran while one was open for 0% of the time, Pallas kernels for 0%

profile of v1, /device:TPU:33, one launch (start us, length us, event | category | flops | bytes accessed | tf_op | source)
XLA Modules:
  0.0 268.2 jit_solution(2638225719243329102)
XLA Ops:
  4.0 1.6 add_reduce_fusion
  8.3 83.0 %all-reduce.6 = (f32[32]{0:T(128)S(1)}, f32[32]{0:T(128)S(1)}) all-reduce(f32[32]{0:T(128)S(1)} %dynamic-update-slice, f32[32]{0:T(128)S(1)} %dynamic-update-slice.3), channel_id=1, replica_groups=mesh['member'=2,'tile'=32,'row'=4,'lev'=2] {'tile'}, use_global_device_ids=true, to_apply=%add | all-reduce | flops 64 | bytes 512
  92.5 1.4 dynamic-update-slice.4
  93.9 1.4 dynamic-update-slice.1
  96.6 8.9 %all-reduce.7 = (f32[4]{0:T(128)S(1)}, f32[4]{0:T(128)S(1)}) all-reduce(f32[4]{0:T(128)S(1)} %dynamic-update-slice.1, f32[4]{0:T(128)S(1)} %dynamic-update-slice.4), channel_id=1, replica_groups=mesh['member'=2,'tile'=32,'row'=4,'lev'=2] {'row'}, use_global_device_ids=true, to_apply=%add.1 | all-reduce | flops 8 | bytes 64
  106.8 1.4 dynamic-update-slice.5
  108.2 1.4 dynamic-update-slice.2
  109.6 18.8 %all-reduce.8 = (f32[2]{0:T(128)S(1)}, f32[2]{0:T(128)S(1)}) all-reduce(f32[2]{0:T(128)S(1)} %dynamic-update-slice.2, f32[2]{0:T(128)S(1)} %dynamic-update-slice.5), channel_id=1, replica_groups=mesh['member'=2,'tile'=32,'row'=4,'lev'=2] {'lev'}, use_global_device_ids=true, to_apply=%add.2 | all-reduce | flops 4 | bytes 32
  133.1 2.0 collective-permute-start
  135.0 4.6 %collective-permute-start.1 = (f32[3,32,8,128]{3,2,1,0:T(8,128)S(1)}, f32[3,32,8,128]{3,2,1,0:T(8,128)}, u32[]{:S(2)}, u32[]{:S(2)}) collective-permute-start(f32[3,32,8,128]{3,2,1,0:T(8,128)S(1)} %get-tuple-element.74), channel_id=1, source_target_pairs={{8,0},{16,8},{24,16},{32,24},{40,32},{48,40},{56,48},{64,56},{72,6... | collective-permute-start | bytes 1179656 | tf_op jit(solution)/shard_map/ppermute | solution.py:31
  139.6 46.2 %pmax.21 = f32[]{:T(128)} all-reduce(f32[]{:T(128)} %get-tuple-element.31), channel_id=1, replica_groups=mesh['member'=2,'tile'=32,'row'=4,'lev'=2] {'tile'}, use_global_device_ids=true, to_apply=%region_9.10 | all-reduce | flops 1 | bytes 8 | tf_op jit(solution)/shard_map/pmax | solution.py:12
  185.9 6.7 %pmax.22 = f32[]{:T(128)} all-reduce(f32[]{:T(128)} %pmax.21), channel_id=1, replica_groups=mesh['member'=2,'tile'=32,'row'=4,'lev'=2] {'row'}, use_global_device_ids=true, to_apply=%region_10.11 | all-reduce | flops 1 | bytes 8 | tf_op jit(solution)/shard_map/pmax | solution.py:12
  192.5 18.6 %pmax.23 = f32[]{:T(128)} all-reduce(f32[]{:T(128)} %pmax.22), channel_id=1, replica_groups=mesh['member'=2,'tile'=32,'row'=4,'lev'=2] {'lev'}, use_global_device_ids=true, to_apply=%region_11.12 | all-reduce | flops 1 | bytes 8 | tf_op jit(solution)/shard_map/pmax | solution.py:12
  215.4 3.6 %collective-permute-start.3 = (f32[3,32,32,8]{2,3,1,0:T(8,128)S(1)}, f32[3,32,32,8]{2,3,1,0:T(8,128)}, u32[]{:S(2)}, u32[]{:S(2)}) collective-permute-start(f32[3,32,32,8]{2,3,1,0:T(8,128)S(1)} %copy.21), channel_id=1, source_target_pairs={{2,0},{4,2},{6,4},{0,6},{3,1},{5,3},{7,5},{1,7},{10,8},{12,10},{14... | collective-permute-start | bytes 294920 | tf_op jit(solution)/shard_map/ppermute | solution.py:31
  219.0 2.1 collective-permute-start.2
  221.2 11.2 %collective-permute-done.2 = f32[3,32,32,8]{2,3,1,0:T(8,128)S(1)} collective-permute-done((f32[3,32,32,8]{2,3,1,0:T(8,128)}, f32[3,32,32,8]{2,3,1,0:T(8,128)S(1)}, u32[]{:S(2)}, u32[]{:S(2)}) %collective-permute-start.2) | collective-permute-done | bytes 98336 | tf_op jit(solution)/shard_map/ppermute | solution.py:28
  232.9 1.5 copy.19
  234.4 2.6 pad_maximum_fusion
  237.3 1.7 slice_multiply_fusion.3
  240.2 1.7 slice_multiply_fusion.1
  247.2 6.2 %all_to_all.5 = f32[2,3,32,16,128]{4,3,2,1,0:T(8,128)S(1)} all-to-all(f32[2,3,32,16,128]{4,3,2,1,0:T(8,128)S(1)} %broadcast_in_dim.2), channel_id=1, replica_groups=mesh['member'=2,'tile'=32,'row'=4,'lev'=2] {'lev'}, dimensions={0} | all-to-all | bytes 3145728 | tf_op jit(solution)/shard_map/all_to_all | solution.py:44
  253.6 6.9 %bitcast_subtract_fusion = f32[64,16,128]{2,1,0:T(8,128)S(1)} fusion(f32[1,2,32,16,128]{4,3,2,0,1:T(8,128)S(1)} %get-tuple-element.62, f32[64,16,128]{2,1,0:T(8,128)S(1)} %bitcast.31), kind=kOutput, calls=%fused_computation.104 | output fusion | flops 8388608 | bytes 1572864 | tf_op jit(solution)/shard_map/jit(cumsum)/reduce_window_sum | solution.py:76
  260.8 2.8 %multiply_reduce_fusion.7 = (f32[33,16,128]{2,1,0:T(8,128)S(1)}, f32[33,16,128]{2,1,0:T(8,128)S(1)}, f32[33,16,128]{2,1,0:T(8,128)S(1)}, f32[33,16,128]{2,1,0:T(...) fusion(f32[8,16,128]{2,1,0:T(8,128)S(1)} %get-tuple-element.82,, ...), kind=kLoop, calls=%fused_computation.8 | loop fusion | flops 14598144 | bytes 3481600 | tf_op jit(solution)/shard_map/reduce_sum | solution.py:86
  263.6 2.7 %multiply_reduce_fusion.6 = (f32[33,16,128]{2,1,0:T(8,128)S(1)}, f32[33,16,128]{2,1,0:T(8,128)S(1)}, f32[33,16,128]{2,1,0:T(8,128)S(1)}, f32[33,16,128]{2,1,0:T(...) fusion(f32[8,16,128]{2,1,0:T(8,128)S(1)} %get-tuple-element.81,, ...), kind=kLoop, calls=%fused_computation.7 | loop fusion | flops 14598144 | bytes 3481600 | tf_op jit(solution)/shard_map/reduce_sum | solution.py:86
  (55 shorter events, 26.2 us)
Async XLA Ops:
  0.6 211.2 %copy-start = (f32[32,16,128]{2,1,0:T(8,128)S(1)}, f32[32,16,128]{2,1,0:T(8,128)}, u32[]{:S(2)}) copy-start(f32[32,16,128]{2,1,0:T(8,128)} %param.6) | copy-start | bytes 786436
  0.6 211.2 %copy-start.1 = (f32[32,16,128]{2,1,0:T(8,128)S(1)}, f32[32,16,128]{2,1,0:T(8,128)}, u32[]{:S(2)}) copy-start(f32[32,16,128]{2,1,0:T(8,128)} %param.5) | copy-start | bytes 786436
  133.1 78.7 %collective-permute-start = (f32[3,32,8,128]{3,2,1,0:T(8,128)S(1)}, f32[3,32,8,128]{3,2,1,0:T(8,128)}, u32[]{:S(2)}, u32[]{:S(2)}) collective-permute-start(f32[3,32,8,128]{3,2,1,0:T(8,128)S(1)} %get-tuple-element.73), channel_id=1, source_target_pairs={{0,8},{8,16},{16,24},{24,32},{32,40},{40,48},{48,56},{56,64},{64,7... | collective-permute-start | bytes 1179656 | tf_op jit(solution)/shard_map/ppermute | solution.py:28
  135.0 76.8 %collective-permute-start.1 = (f32[3,32,8,128]{3,2,1,0:T(8,128)S(1)}, f32[3,32,8,128]{3,2,1,0:T(8,128)}, u32[]{:S(2)}, u32[]{:S(2)}) collective-permute-start(f32[3,32,8,128]{3,2,1,0:T(8,128)S(1)} %get-tuple-element.74), channel_id=1, source_target_pairs={{8,0},{16,8},{24,16},{32,24},{40,32},{48,40},{56,48},{64,56},{72,6... | collective-permute-start | bytes 1179656 | tf_op jit(solution)/shard_map/ppermute | solution.py:31
  215.4 17.5 %collective-permute-start.3 = (f32[3,32,32,8]{2,3,1,0:T(8,128)S(1)}, f32[3,32,32,8]{2,3,1,0:T(8,128)}, u32[]{:S(2)}, u32[]{:S(2)}) collective-permute-start(f32[3,32,32,8]{2,3,1,0:T(8,128)S(1)} %copy.21), channel_id=1, source_target_pairs={{2,0},{4,2},{6,4},{0,6},{3,1},{5,3},{7,5},{1,7},{10,8},{12,10},{14... | collective-permute-start | bytes 294920 | tf_op jit(solution)/shard_map/ppermute | solution.py:31
  219.0 13.4 %collective-permute-start.2 = (f32[3,32,32,8]{2,3,1,0:T(8,128)}, f32[3,32,32,8]{2,3,1,0:T(8,128)S(1)}, u32[]{:S(2)}, u32[]{:S(2)}) collective-permute-start(f32[3,32,32,8]{2,3,1,0:T(8,128)} %copy.20), channel_id=1, source_target_pairs={{0,2},{2,4},{4,6},{6,0},{1,3},{3,5},{5,7},{7,1},{8,10},{10,12},{12... | collective-permute-start | bytes 294920 | tf_op jit(solution)/shard_map/ppermute | solution.py:28
